TPU v7x, 256 devices: a whole 4x4x8 slice. The times are simulated.
256 devices in a mesh: prow: 32 (over x, z), pcol: 8 (over y, core).
Axes of the slice: x: 4, y: 4, z: 8, core: 2. Of those that a mesh axis runs over, the one named last changes fastest.
Arguments:
- inverse_pool: float32 [12288, 12288], P('prow', 'pcol'), may hold values from -6 to 6
- panel_one: float32 [12288, 512], P(('prow', 'pcol')), may hold values from -0.0625 to 0.0625
- panel_two: float32 [12288, 512], P(('prow', 'pcol')), may hold values from -0.078125 to 0.078125
- upper_two: float32 [512, 512], replicated, may hold values from -0.25 to 0.25
- lower_one: float32 [512, 512], replicated, as said below
- lower_two: float32 [512, 512], replicated, as said below
- list_one: int32 [72], replicated, may hold values from 0 to 95, as said below
- list_two: int32 [48], replicated, may hold values from 0 to 95, as said below
Outputs:
- first_offdiag: float32 [12288, 512], P(('prow', 'pcol'))
- first_diag: float32 [512, 512], replicated
- second_offdiag: float32 [12288, 512], P(('prow', 'pcol'))
- second_coupling: float32 [512, 512], replicated
- second_diag: float32 [512, 512], replicated
Inputs may be any that keep to these rules, and one draw needn't show every extreme that they name: `list_one`: distinct block numbers, among them 0, 48 and 95. `list_two`: distinct block numbers, each of which is also in list_one, among them 0, 48 and 95. `lower_one`: lower triangular with a diagonal of 1 to 1.5. `lower_two`: lower triangular with a diagonal of 1 to 1.5.
All inputs are finite; a program needn't handle non-finite values.
Results may differ from a plain program's by a relative error of at most 0.000073.
Values sent between devices are 32-bit elements; how exact they have to be, the bound alone decides.
No kernel may reach another device: no remote copies, remote signals or barrier semaphores. Data moves between devices by JAX's collectives and lax.ppermute only.
A program may use at most 64 MiB of HBM per device.

v0:
```python
import jax
import jax.numpy as jnp
from jax import lax
from jax.sharding import Mesh
from jax.sharding import PartitionSpec as P

BLK = 128
PROW = ("prow_0", "prow_1")
PCOL = ("pcol_0", "pcol_1")
PROW_PCOL = ("prow_0", "prow_1", "pcol_0", "pcol_1")


def laid_out(parts, dim):
    shape = list(parts.shape[1:])
    shape[dim] *= parts.shape[0]
    return jnp.moveaxis(parts, 0, dim).reshape(shape)


def stacked_from(x, axes, turns):
    parts = x[None]
    for k in turns:
        parts = lax.all_gather(parts, axes[k], axis=0, tiled=True)
    carried = [lax.axis_size(axes[k]) for k in reversed(turns)]
    parts = parts.reshape(*carried, *x.shape)
    turned = sorted(range(len(turns)), key=lambda place: turns[len(turns) - 1 - place])
    return parts.transpose(*turned, *range(len(turns), parts.ndim)).reshape(-1, *x.shape)


def whole_of(x, axes, turns, dim):
    return laid_out(stacked_from(x, axes, turns), dim)


def in_blocks(x, dim, count):
    shape = x.shape
    parts = x.reshape(*shape[:dim], count, shape[dim] // count, *shape[dim + 1 :])
    return jnp.moveaxis(parts, dim, 0)


def summed_on_arrival(x, axis, dim):
    count = lax.axis_size(axis)
    parts = lax.all_to_all(in_blocks(x, dim, count), axis, 0, 0, tiled=True)
    return jnp.sum(parts, axis=0)


def summed_rows(x, axes, dim):
    far, near = axes
    parts = in_blocks(x, dim, lax.axis_size(far))
    nearer = summed_on_arrival(parts, near, dim + 1)
    arrived = lax.all_to_all(nearer, far, split_axis=0, concat_axis=0, tiled=True)
    return arrived.sum(axis=0)


def rows_for(lines, count):
    spare = -lines.shape[0] % count
    if not spare:
        return lines
    return jnp.concatenate([lines, jnp.zeros((spare, *lines.shape[1:]), lines.dtype)])


def from_everyone(x, axis):
    copies = jnp.broadcast_to(x, (lax.axis_size(axis), *x.shape))
    return lax.all_to_all(copies, axis, split_axis=0, concat_axis=0, tiled=True)


def whole_of_2(x, axes, dim):
    far, near = axes
    leading = from_everyone(x, far)
    parts = jnp.swapaxes(from_everyone(leading, near), 0, 1)
    return laid_out(parts.reshape(-1, *x.shape), dim)


def nested_sum(x, axes):
    own = summed_rows(rows_for(x, lax.axis_size(axes[0]) * lax.axis_size(axes[1])), axes, 0)
    whole = whole_of_2(own, axes, 0)
    return whole[: len(x)].reshape(x.shape)


def together(arrays, axis):
    ends = [0]
    for a in arrays:
        ends.append(ends[-1] + a.size)
    total = nested_sum(jnp.concatenate([a.ravel() for a in arrays]), axis)
    return tuple((total[b:e].reshape(a.shape) for a, b, e in zip(arrays, ends, ends[1:])))


def product(left, right):
    return jnp.dot(left, right, precision=lax.Precision.HIGHEST, preferred_element_type=jnp.float32)


def transposed_product(left, right):
    return lax.dot_general(
        left,
        right,
        (((0,), (0,)), ((), ())),
        precision=lax.Precision.HIGHEST,
        preferred_element_type=jnp.float32,
    )


def live_rows(listing, first_row, count):
    row_ids = first_row + lax.iota(jnp.int32, count)
    blocks = row_ids // BLK
    hits = jnp.any(blocks[:, None] == listing[None, :], axis=1)
    return jnp.where(hits, 1.0, 0.0).astype(jnp.float32)[:, None]


def multiply_ancestors(inverse_tile, masked_span):
    groups = lax.axis_size(PROW) // lax.axis_size(PCOL)
    columns = lax.axis_size(PCOL)
    span_rows = masked_span.shape[0]
    stacked = whole_of(masked_span, PROW, (0, 1), 0)
    grouped = stacked.reshape(columns, groups * span_rows, masked_span.shape[1])
    regrouped = lax.all_to_all(grouped, PCOL, split_axis=0, concat_axis=0, tiled=True)
    accumulated = jnp.einsum(
        "rjkm,kjmw->rw",
        inverse_tile.reshape(inverse_tile.shape[0], groups, columns, span_rows),
        regrouped.reshape(columns, groups, span_rows, masked_span.shape[1]),
        precision=lax.Precision.HIGHEST,
        preferred_element_type=jnp.float32,
    )
    return summed_on_arrival(accumulated, PCOL, 0)


def local(inverse_pool, panel_one, panel_two, upper_two, lower_one, lower_two, list_one, list_two):
    span_rows = panel_one.shape[0]
    span_index = lax.axis_index(PROW) * lax.axis_size(PCOL) + lax.axis_index(PCOL)
    first_row = span_index * span_rows
    live_one = live_rows(list_one, first_row, span_rows)
    live_two = live_rows(list_two, first_row, span_rows)
    masked_one = live_one * panel_one
    masked_two = live_two * panel_two
    first_offdiag = -live_one * multiply_ancestors(inverse_pool, masked_one)
    second_product = multiply_ancestors(inverse_pool, masked_two)
    second_offdiag = -live_two * (product(first_offdiag, upper_two) + second_product)
    first_terms, coupling_terms, last_terms = together(
        (
            transposed_product(masked_one, first_offdiag),
            transposed_product(first_offdiag, masked_two),
            transposed_product(masked_two, second_offdiag),
        ),
        (("prow_0", "prow_1"), ("pcol_0", "pcol_1")),
    )
    first_diag = transposed_product(lower_one, lower_one) - first_terms
    second_coupling = -(product(first_diag, upper_two) + coupling_terms)
    second_diag = (
        transposed_product(lower_two, lower_two)
        - transposed_product(upper_two, second_coupling)
        - last_terms
    )
    return (first_offdiag, first_diag, second_offdiag, second_coupling, second_diag)


def solution(mesh):
    finer = Mesh(mesh.devices.reshape(4, 8, 4, 2), ("prow_0", "prow_1", "pcol_0", "pcol_1"))
    placed = (P(PROW, PCOL), P(PROW_PCOL, None), P(PROW_PCOL, None), P(), P(), P(), P(), P())
    return jax.shard_map(
        local,
        mesh=finer,
        in_specs=placed,
        out_specs=(P(PROW_PCOL, None), P(), P(PROW_PCOL, None), P(), P()),
        check_vma=False,
    )
```

profile of v0, /device:TPU:1, one launch (start us, length us, event | category | flops | bytes accessed | tf_op | source)
XLA Modules:
  0.0 368.6 jit_solution(7397864533906607054)
XLA Ops:
  7.2 0.0 copy-start
  7.2 0.0 all-gather.5.cloned.1.call-start
  7.3 0.9 compare_reduce_fusion.1
  8.2 1.0 broadcast_multiply_fusion.1
  9.2 0.6 copy-done.7
  9.8 12.3 %all-gather = f32[192,512]{1,0:T(8,128)} all-gather(f32[48,512]{1,0:T(8,128)S(1)} %broadcast_multiply_fusion.1), channel_id=2, replica_groups=mesh['prow_0'=4,'prow_1'=8,'pcol_0'=4,'pcol_1'=2] {'prow_0'}, dimensions={0}, use_global_device_ids=true | all-gather | bytes 491520 | tf_op jit(solution)/shard_map/all_gather | solution.py:22
  22.1 0.0 all-gather.5.cloned.1.call-update
  22.1 0.0 all-gather.7.cloned.1.call-start
  22.2 0.8 compare_reduce_fusion
  23.0 1.0 broadcast_multiply_fusion
  24.0 10.4 %all-gather.1 = f32[192,512]{1,0:T(8,128)} all-gather(f32[48,512]{1,0:T(8,128)S(1)} %broadcast_multiply_fusion), channel_id=3, replica_groups=mesh['prow_0'=4,'prow_1'=8,'pcol_0'=4,'pcol_1'=2] {'prow_0'}, dimensions={0}, use_global_device_ids=true | all-gather | bytes 491520 | tf_op jit(solution)/shard_map/all_gather | solution.py:22
  34.4 0.0 all-gather.7.cloned.1.call-update
  34.4 37.2 %all-gather.5.cloned.1.call-done = f32[32,48,512]{2,1,0:T(8,128)} async-done(((f32[4,48,512]{2,1,0:T(8,128)}), f32[32,48,512]{2,1,0:T(8,128)}) %all-gather.5.cloned.1.call-update) | async-done | bytes 3145744 | tf_op jit(solution)/shard_map/all_gather | solution.py:22
  71.6 4.1 %copy.41 = f32[4,8,48,512]{3,2,1,0:T(8,128)} copy(f32[4,8,48,512]{3,2,0,1:T(8,128)} %bitcast.75) | data formatting | bytes 6291456 | tf_op jit(solution)/shard_map/transpose | solution.py:26
  75.7 5.6 %all-to-all-start = ((f32[8,192,512]{2,1,0:T(8,128)}), f32[8,192,512]{2,1,0:T(8,128)}, u32[]{:S(2)}, u32[]{:S(2)}) async-start(f32[8,192,512]{2,1,0:T(8,128)} %bitcast.68), calls=%async_computation | async-start | bytes 6291456 | tf_op jit(solution)/shard_map/all_to_all | solution.py:113
  81.3 35.8 %all-gather.7.cloned.1.call-done = f32[32,48,512]{2,1,0:T(8,128)} async-done(((f32[4,48,512]{2,1,0:T(8,128)}), f32[32,48,512]{2,1,0:T(8,128)}) %all-gather.7.cloned.1.call-update) | async-done | bytes 3145744 | tf_op jit(solution)/shard_map/all_gather | solution.py:22
  117.1 4.0 %copy.44 = f32[4,8,48,512]{3,2,1,0:T(8,128)} copy(f32[4,8,48,512]{3,2,0,1:T(8,128)} %bitcast.76) | data formatting | bytes 6291456 | tf_op jit(solution)/shard_map/transpose | solution.py:26
  121.1 0.0 all-to-all-done
  121.1 5.6 %all-to-all-start.2 = ((f32[8,192,512]{2,1,0:T(8,128)}), f32[8,192,512]{2,1,0:T(8,128)}, u32[]{:S(2)}, u32[]{:S(2)}) async-start(f32[8,192,512]{2,1,0:T(8,128)} %bitcast.67), calls=%async_computation.2 | async-start | bytes 6291456 | tf_op jit(solution)/shard_map/all_to_all | solution.py:113
  126.7 2.0 copy.42
  128.7 6.8 %fusion.2 = f32[512,384,1,1]{0,1,3,2:T(8,128)} fusion(f32[384,4,8,48]{0,3,2,1:T(8,128)S(1)} %bitcast.65, f32[8,4,48,512]{3,2,1,0:T(8,128)} %bitcast.4), kind=kOutput, calls=%fused_computation.3 | convolution fusion | flops 3623878656 | bytes 6291456 | tf_op jit(solution)/shard_map/rjkm,kjmw->rw/dot_general | solution.py:114
  135.5 28.8 %all-to-all-done.2 = f32[8,192,512]{2,1,0:T(8,128)} async-done(((f32[8,192,512]{2,1,0:T(8,128)}), f32[8,192,512]{2,1,0:T(8,128)}, u32[]{:S(2)}, u32[]{:S(2)}) %all-to-all-start.2) | async-done | bytes 3145760 | tf_op jit(solution)/shard_map/all_to_all | solution.py:113
  164.2 5.1 %all-to-all-start.1 = ((f32[8,48,512]{2,1,0:T(8,128)}), f32[8,48,512]{2,1,0:T(8,128)}, u32[]{:S(2)}, u32[]{:S(2)}) async-start(f32[8,48,512]{2,1,0:T(8,128)} %bitcast.74), calls=%async_computation.1 | async-start | bytes 1572864 | tf_op jit(solution)/shard_map/all_to_all | solution.py:41
  169.3 6.8 %fusion = f32[512,384,1,1]{0,1,3,2:T(8,128)} fusion(f32[384,4,8,48]{0,3,2,1:T(8,128)S(1)} %bitcast.66, f32[8,4,48,512]{3,2,1,0:T(8,128)} %bitcast.14), kind=kOutput, calls=%fused_computation.1 | convolution fusion | flops 3623878656 | bytes 6291456 | tf_op jit(solution)/shard_map/rjkm,kjmw->rw/dot_general | solution.py:114
  176.1 5.5 %all-to-all-done.1 = f32[8,48,512]{2,1,0:T(8,128)} async-done(((f32[8,48,512]{2,1,0:T(8,128)}), f32[8,48,512]{2,1,0:T(8,128)}, u32[]{:S(2)}, u32[]{:S(2)}) %all-to-all-start.1) | async-done | bytes 786464 | tf_op jit(solution)/shard_map/all_to_all | solution.py:41
  181.6 5.1 %all-to-all-start.3 = ((f32[8,48,512]{2,1,0:T(8,128)}), f32[8,48,512]{2,1,0:T(8,128)}, u32[]{:S(2)}, u32[]{:S(2)}) async-start(f32[8,48,512]{2,1,0:T(8,128)} %bitcast.73), calls=%async_computation.3 | async-start | bytes 1572864 | tf_op jit(solution)/shard_map/all_to_all | solution.py:41
  186.7 1.2 reduce_sum.36
  187.9 0.1 broadcast_multiply_fusion.2
  187.9 1.0 convolution_bitcast_fusion.2
  189.0 0.0 copy-done.8
  189.0 1.0 convolution_bitcast_fusion.3
  190.0 8.9 %all-to-all-done.3 = f32[8,48,512]{2,1,0:T(8,128)} async-done(((f32[8,48,512]{2,1,0:T(8,128)}), f32[8,48,512]{2,1,0:T(8,128)}, u32[]{:S(2)}, u32[]{:S(2)}) %all-to-all-start.3) | async-done | bytes 786464 | tf_op jit(solution)/shard_map/all_to_all | solution.py:41
  199.0 1.8 reduce_sum.37
  200.8 0.0 copy-done
  200.8 1.6 fusion.7
  202.4 0.0 copy-start.9
  202.4 1.0 convolution_bitcast_fusion.1
  203.5 0.3 copy.55
  203.8 0.3 copy.54
  204.0 0.3 copy.53
  204.3 0.0 copy-done.9
  204.3 1.8 pad_maximum_fusion
  206.2 4.5 %reshape_reshape.4 = f32[32,8,3072]{2,1,0:T(8,128)} reshape(f32[786432]{0:T(1024)} %pad_maximum_fusion) | data formatting | bytes 6291456 | tf_op jit(solution)/shard_map/reshape;reshape | solution.py:35
  210.7 3.7 %copy.46 = f32[8,32,3072]{2,1,0:T(8,128)S(1)} copy(f32[8,32,3072]{2,0,1:T(8,128)} %bitcast.69) | data formatting | bytes 6291456 | tf_op jit(solution)/shard_map/transpose | solution.py:36
  214.4 41.6 %all_to_all.48 = f32[8,32,3072]{2,1,0:T(8,128)} all-to-all(f32[8,32,3072]{2,1,0:T(8,128)S(1)} %copy.46), channel_id=1, replica_groups=mesh['prow_0'=4,'prow_1'=8,'pcol_0'=4,'pcol_1'=2] {'pcol_0','pcol_1'}, dimensions={0} | all-to-all | bytes 6291456 | tf_op jit(solution)/shard_map/all_to_all | solution.py:41
  256.0 2.1 reduce_sum.38
  258.1 0.3 all_to_all.35
  258.3 17.6 %all_to_all.49 = f32[32,1,3072]{2,1,0:T(1,128)S(1)} all-to-all(f32[32,1,3072]{2,1,0:T(1,128)S(1)} %all_to_all.35), channel_id=1, replica_groups=mesh['prow_0'=4,'prow_1'=8,'pcol_0'=4,'pcol_1'=2] {'prow_0','prow_1'}, dimensions={0} | all-to-all | bytes 786432 | tf_op jit(solution)/shard_map/all_to_all | solution.py:49
  275.9 0.2 reduce_sum.39
  276.2 0.2 broadcast_in_dim.32
  276.4 18.1 %all_to_all.50 = f32[32,1,3072]{2,1,0:T(1,128)S(1)} all-to-all(f32[32,1,3072]{2,1,0:T(1,128)S(1)} %broadcast_in_dim.32), channel_id=1, replica_groups=mesh['prow_0'=4,'prow_1'=8,'pcol_0'=4,'pcol_1'=2] {'prow_0','prow_1'}, dimensions={0} | all-to-all | bytes 786432 | tf_op jit(solution)/shard_map/all_to_all | solution.py:62
  294.5 0.1 copy.61
  294.6 2.0 broadcast_in_dim.33
  296.6 9.4 %all-to-all-start.7 = ((f32[8,32,3072]{2,1,0:T(8,128)}), f32[8,32,3072]{2,1,0:T(8,128)}, u32[]{:S(2)}, u32[]{:S(2)}) async-start(f32[8,32,3072]{2,1,0:T(8,128)} %broadcast_in_dim.33), calls=%async_computation.7 | async-start | bytes 6291456 | tf_op jit(solution)/shard_map/all_to_all | solution.py:62
  306.0 1.9 fusion.10
  307.9 35.7 %all-to-all-done.7 = f32[8,32,3072]{2,1,0:T(8,128)} async-done(((f32[8,32,3072]{2,1,0:T(8,128)}), f32[8,32,3072]{2,1,0:T(8,128)}, u32[]{:S(2)}, u32[]{:S(2)}) %all-to-all-start.7) | async-done | bytes 3145760 | tf_op jit(solution)/shard_map/all_to_all | solution.py:62
  343.6 5.4 %copy.47 = f32[32,8,3072]{2,1,0:T(8,128)} copy(f32[32,8,3072]{2,0,1:T(8,128)} %bitcast.20) | data formatting | bytes 6291456 | tf_op jit(solution)/shard_map/transpose | solution.py:68
  349.0 4.7 %slice.14 = f32[1536,512]{1,0:T(8,128)} reshape(f32[32,8,3072]{2,1,0:T(8,128)} %copy.47) | data formatting | bytes 6291456 | tf_op jit(solution)/shard_map/slice | solution.py:83
  353.7 0.0 copy-done.3
  353.7 3.3 convolution_subtract_fusion
  357.0 0.0 copy-start.5
  357.0 1.9 fusion.6
  358.8 0.0 copy-start.4
  358.9 2.9 fusion.5
  (14 shorter events, 0.0 us)
Async XLA Ops:
  7.2 193.6 %copy-start = (f32[512,512]{1,0:T(8,128)S(1)}, f32[512,512]{1,0:T(8,128)}, u32[]{:S(2)}) copy-start(f32[512,512]{1,0:T(8,128)} %param.11) | copy-start | bytes 3145732
  7.2 64.5 %all-gather.5.cloned.1.call-start = ((), (), s32[]{:S(2)}) async-start(), calls=%async_computation.8 | async-start | bytes 3538944 | tf_op jit(solution)/shard_map/all_gather | solution.py:22
  9.2 0.6 copy-start.7
  22.1 95.0 %all-gather.7.cloned.1.call-start = ((), (), s32[]{:S(2)}) async-start(), calls=%async_computation.9 | async-start | bytes 3538944 | tf_op jit(solution)/shard_map/all_gather | solution.py:22
  75.7 45.4 %all-to-all-start = ((f32[8,192,512]{2,1,0:T(8,128)}), f32[8,192,512]{2,1,0:T(8,128)}, u32[]{:S(2)}, u32[]{:S(2)}) async-start(f32[8,192,512]{2,1,0:T(8,128)} %bitcast.68), calls=%async_computation | async-start | bytes 6291456 | tf_op jit(solution)/shard_map/all_to_all | solution.py:113
  121.1 43.1 %all-to-all-start.2 = ((f32[8,192,512]{2,1,0:T(8,128)}), f32[8,192,512]{2,1,0:T(8,128)}, u32[]{:S(2)}, u32[]{:S(2)}) async-start(f32[8,192,512]{2,1,0:T(8,128)} %bitcast.67), calls=%async_computation.2 | async-start | bytes 6291456 | tf_op jit(solution)/shard_map/all_to_all | solution.py:113
  164.2 17.4 %all-to-all-start.1 = ((f32[8,48,512]{2,1,0:T(8,128)}), f32[8,48,512]{2,1,0:T(8,128)}, u32[]{:S(2)}, u32[]{:S(2)}) async-start(f32[8,48,512]{2,1,0:T(8,128)} %bitcast.74), calls=%async_computation.1 | async-start | bytes 1572864 | tf_op jit(solution)/shard_map/all_to_all | solution.py:41
  176.1 12.9 %copy-start.8 = (f32[48,512]{1,0:T(8,128)S(1)}, f32[48,512]{1,0:T(8,128)}, u32[]{:S(2)}) copy-start(f32[48,512]{1,0:T(8,128)} %copy-done.7) | copy-start | bytes 294916
  181.6 17.4 %all-to-all-start.3 = ((f32[8,48,512]{2,1,0:T(8,128)}), f32[8,48,512]{2,1,0:T(8,128)}, u32[]{:S(2)}, u32[]{:S(2)}) async-start(f32[8,48,512]{2,1,0:T(8,128)} %bitcast.73), calls=%async_computation.3 | async-start | bytes 1572864 | tf_op jit(solution)/shard_map/all_to_all | solution.py:41
  187.9 15.8 %copy-start.6 = (f32[48,512]{1,0:T(8,128)}, f32[48,512]{1,0:T(8,128)S(1)}, u32[]{:S(2)}) copy-start(f32[48,512]{1,0:T(8,128)S(1)} %broadcast_multiply_fusion.2) | copy-start | bytes 294916
  202.4 1.9 copy-start.9
  296.6 9.4 %copy-start.2 = (f32[512,512]{1,0:T(8,128)S(1)}, f32[512,512]{1,0:T(8,128)}, u32[]{:S(2)}) copy-start(f32[512,512]{1,0:T(8,128)} %param.13) | copy-start | bytes 3145732
  296.6 47.0 %all-to-all-start.7 = ((f32[8,32,3072]{2,1,0:T(8,128)}), f32[8,32,3072]{2,1,0:T(8,128)}, u32[]{:S(2)}, u32[]{:S(2)}) async-start(f32[8,32,3072]{2,1,0:T(8,128)} %broadcast_in_dim.33), calls=%async_computation.7 | async-start | bytes 6291456 | tf_op jit(solution)/shard_map/all_to_all | solution.py:62
  349.0 4.7 %copy-start.3 = (f32[512,512]{1,0:T(8,128)S(1)}, f32[512,512]{1,0:T(8,128)}, u32[]{:S(2)}) copy-start(f32[512,512]{1,0:T(8,128)} %param.12) | copy-start | bytes 3145732
  353.7 3.3 copy-start.1
  357.0 4.8 %copy-start.5 = (f32[512,512]{1,0:T(8,128)}, f32[512,512]{1,0:T(8,128)S(1)}, u32[]{:S(2)}) copy-start(f32[512,512]{1,0:T(8,128)S(1)} %convolution_subtract_fusion) | copy-start | bytes 3145732
  358.8 2.9 copy-start.4
Sparse Core Ops, SparseCore 0:
  22.2 49.3 all-gather.4
  73.4 43.5 all-gather.6
where the time goes:
time: 370 us; the launch traced here: 369 us
  waiting for transfers between devices  152 us (41%)
  blocking collectives  100 us (27%)
  local copies, waits for them, and re-layouts  32.6 us (9%)
  starting transfers between devices  30.7 us (8%)
  matrix products  28 us (8%)
  between operations  14.3 us (4%)
  other arithmetic  11 us (3%)
    all_gather x2, waiting for transfers between devices, stacked_from(): parts = lax.all_gather(parts, axes[k], axis=0, tiled=True)  73 us
    all_to_all x1, blocking collectives, summed_on_arrival(): parts = lax.all_to_all(in_blocks(x, dim, count), axis, 0, 0, tiled=True)  41.6 us
    all_to_all x1, waiting for transfers between devices, from_everyone(): return lax.all_to_all(copies, axis, split_axis=0, concat_axis=0, tiled=True)  35.7 us
    all_to_all x2, waiting for transfers between devices, multiply_ancestors(): lax.all_to_all(grouped, PCOL, split_axis=0, concat_axis=0, tiled=True)  28.8 us
    all_gather x2, blocking collectives, stacked_from(): parts = lax.all_gather(parts, axes[k], axis=0, tiled=True)  22.7 us
    all_to_all x1, blocking collectives, from_everyone(): return lax.all_to_all(copies, axis, split_axis=0, concat_axis=0, tiled=True)  18.1 us
    all_to_all x1, blocking collectives, summed_rows(): lax.all_to_all(nearer, far, split_axis=0, concat_axis=0, tiled=True)  17.6 us
    all_to_all x2, waiting for transfers between devices, summed_on_arrival(): parts = lax.all_to_all(in_blocks(x, dim, count), axis, 0, 0, tiled=True)  14.5 us
  transfers between devices with their start and end apart: 7, of which 6 were waited for; matrix products, arithmetic and copies ran while one was open for 8% of the time, Pallas kernels for 0%

commit v1 on v0

--- a/solution.py
+++ b/solution.py
@@ -19,7 +19,9 @@
 def stacked_from(x, axes, turns):
     parts = x[None]
     for k in turns:
-        parts = lax.all_gather(parts, axes[k], axis=0, tiled=True)
+        parts = jnp.concatenate(
+            lax.all_to_all(jnp.stack([parts] * lax.axis_size(axes[k])), axes[k], 0, 0), axis=0
+        )
     carried = [lax.axis_size(axes[k]) for k in reversed(turns)]
     parts = parts.reshape(*carried, *x.shape)
     turned = sorted(range(len(turns)), key=lambda place: turns[len(turns) - 1 - place])

time: 370 us -> 464 us (1.25)
  blocking collectives: 100 us -> 161 us
  waiting for transfers between devices: 152 us -> 182 us
  between operations: 14.3 us -> 0.9 us
  starting transfers between devices: 30.7 us -> 44 us
    all_to_all x0 -> x2, blocking collectives: none -> 86.7 us  [stacked_from(): lax.all_to_all(jnp.stack([parts] * lax.axis_size(axes[k])), axes[k], 0, 0)]
    all_gather x2 -> x0, waiting for transfers between devices: 73 us -> none  [stacked_from(): parts = lax.all_gather(parts, axes[k], axis=0, tiled=True)]
    all_to_all x0 -> x2, waiting for transfers between devices: none -> 69.2 us  [stacked_from(): lax.all_to_all(jnp.stack([parts] * lax.axis_size(axes[k])), axes[k], 0, 0)]
    all_to_all x2, waiting for transfers between devices: 28.8 us -> 62.3 us  [multiply_ancestors(): lax.all_to_all(grouped, PCOL, split_axis=0, concat_axis=0, tiled=True)]
    all_gather x2 -> x0, blocking collectives: 22.7 us -> none  [stacked_from(): parts = lax.all_gather(parts, axes[k], axis=0, tiled=True)]
    all_to_all x0 -> x2, starting transfers between devices: none -> 9.27 us  [stacked_from(): lax.all_to_all(jnp.stack([parts] * lax.axis_size(axes[k])), axes[k], 0, 0)]
    transpose x2 -> x0, local copies, waits for them, and re-layouts: 8.14 us -> none  [stacked_from(): parts.transpose(*turned, *range(len(turns), parts.ndim))]
    all_to_all x0 -> x2, local copies, waits for them, and re-layouts: none -> 8.1 us  [stacked_from(): lax.all_to_all(jnp.stack([parts] * lax.axis_size(axes[k])), axes[k], 0, 0)]
  transfers between devices with their start and end apart: 7 -> 7, of which waited for: 6 -> 7; matrix products, arithmetic and copies ran while one was open for 8% -> 7% of each run, Pallas kernels for 0% -> 0%
where the time goes in v1:
time: 464 us; the launch traced here: 462 us
  waiting for transfers between devices  182 us (39%)
  blocking collectives  161 us (35%)
  starting transfers between devices  44 us (9%)
  local copies, waits for them, and re-layouts  35.8 us (8%)
  matrix products  28 us (6%)
  other arithmetic  11 us (2%)
    all_to_all x2, blocking collectives, stacked_from(): lax.all_to_all(jnp.stack([parts] * lax.axis_size(axes[k])), axes[k], 0, 0)  86.7 us
    all_to_all x2, waiting for transfers between devices, stacked_from(): lax.all_to_all(jnp.stack([parts] * lax.axis_size(axes[k])), axes[k], 0, 0)  69.2 us
    all_to_all x2, waiting for transfers between devices, multiply_ancestors(): lax.all_to_all(grouped, PCOL, split_axis=0, concat_axis=0, tiled=True)  62.3 us
    all_to_all x1, blocking collectives, summed_on_arrival(): parts = lax.all_to_all(in_blocks(x, dim, count), axis, 0, 0, tiled=True)  41.6 us
    all_to_all x1, waiting for transfers between devices, from_everyone(): return lax.all_to_all(copies, axis, split_axis=0, concat_axis=0, tiled=True)  35.7 us
    all_to_all x1, blocking collectives, from_everyone(): return lax.all_to_all(copies, axis, split_axis=0, concat_axis=0, tiled=True)  18.1 us
    all_to_all x2, starting transfers between devices, multiply_ancestors(): lax.all_to_all(grouped, PCOL, split_axis=0, concat_axis=0, tiled=True)  15.6 us
    all_to_all x1, blocking collectives, summed_rows(): lax.all_to_all(nearer, far, split_axis=0, concat_axis=0, tiled=True)  14.6 us
  transfers between devices with their start and end apart: 7, of which 7 were waited for; matrix products, arithmetic and copies ran while one was open for 7% of the time, Pallas kernels for 0%

profile of v1, /device:TPU:1, one launch (start us, length us, event | category | flops | bytes accessed | tf_op | source)
XLA Modules:
  0.0 462.3 jit_solution(5653758553585730392)
XLA Ops:
  0.6 0.0 copy-start
  0.7 0.9 compare_reduce_fusion.1
  1.6 1.0 broadcast_multiply_fusion.1
  2.6 0.6 copy-done.7
  3.2 0.8 stack.12
  4.0 4.8 %all-to-all-start = ((f32[4,1,48,512]{3,2,1,0:T(8,128)}), f32[4,1,48,512]{3,2,1,0:T(8,128)S(1)}, u32[]{:S(2)}, u32[]{:S(2)}) async-start(f32[4,1,48,512]{3,2,1,0:T(8,128)} %stack.12), calls=%async_computation | async-start | bytes 786432 | tf_op jit(solution)/shard_map/all_to_all | solution.py:23
  8.8 0.8 compare_reduce_fusion
  9.7 1.0 broadcast_multiply_fusion
  10.7 4.4 all-to-all-done
  15.1 8.6 %all_to_all.68 = f32[4,1,48,512]{3,2,1,0:T(8,128)S(1)} all-to-all(f32[4,1,48,512]{3,2,1,0:T(8,128)S(1)} %stack.14), channel_id=1, replica_groups=mesh['prow_0'=4,'prow_1'=8,'pcol_0'=4,'pcol_1'=2] {'prow_0'}, dimensions={0} | all-to-all | bytes 786432 | tf_op jit(solution)/shard_map/all_to_all | solution.py:23
  23.7 0.4 stack.13
  24.1 78.1 %all_to_all.69 = f32[8,4,48,512]{3,2,1,0:T(8,128)} all-to-all(f32[8,4,48,512]{3,2,1,0:T(8,128)S(1)} %stack.13), channel_id=1, replica_groups=mesh['prow_0'=4,'prow_1'=8,'pcol_0'=4,'pcol_1'=2] {'prow_1'}, dimensions={0} | all-to-all | bytes 6291456 | tf_op jit(solution)/shard_map/all_to_all | solution.py:23
  102.2 2.0 stack.15
  104.3 4.4 all-to-all-start.5
  108.7 4.1 copy.35
  112.8 64.8 %all-to-all-done.5 = f32[8,4,48,512]{3,2,1,0:T(8,128)} async-done(((f32[8,4,48,512]{3,2,1,0:T(8,128)}), f32[8,4,48,512]{3,2,1,0:T(8,128)}, u32[]{:S(2)}, u32[]{:S(2)}) %all-to-all-start.5) | async-done | bytes 3145760 | tf_op jit(solution)/shard_map/all_to_all | solution.py:23
  177.5 10.3 %all-to-all-start.2 = ((f32[8,192,512]{2,1,0:T(8,128)}), f32[8,192,512]{2,1,0:T(8,128)}, u32[]{:S(2)}, u32[]{:S(2)}) async-start(f32[8,192,512]{2,1,0:T(8,128)} %bitcast.66), calls=%async_computation.2 | async-start | bytes 6291456 | tf_op jit(solution)/shard_map/all_to_all | solution.py:115
  187.8 4.0 copy.38
  191.9 33.5 %all-to-all-done.2 = f32[8,192,512]{2,1,0:T(8,128)} async-done(((f32[8,192,512]{2,1,0:T(8,128)}), f32[8,192,512]{2,1,0:T(8,128)}, u32[]{:S(2)}, u32[]{:S(2)}) %all-to-all-start.2) | async-done | bytes 3145760 | tf_op jit(solution)/shard_map/all_to_all | solution.py:115
  225.4 5.3 %all-to-all-start.6 = ((f32[8,192,512]{2,1,0:T(8,128)}), f32[8,192,512]{2,1,0:T(8,128)}, u32[]{:S(2)}, u32[]{:S(2)}) async-start(f32[8,192,512]{2,1,0:T(8,128)} %bitcast.65), calls=%async_computation.6 | async-start | bytes 6291456 | tf_op jit(solution)/shard_map/all_to_all | solution.py:115
  230.7 2.0 copy.36
  232.7 6.8 %fusion.2 = f32[512,384,1,1]{0,1,3,2:T(8,128)} fusion(f32[384,4,8,48]{0,3,2,1:T(8,128)S(1)} %bitcast.63, f32[8,4,48,512]{3,2,1,0:T(8,128)} %bitcast.3), kind=kOutput, calls=%fused_computation.3 | convolution fusion | flops 3623878656 | bytes 6291456 | tf_op jit(solution)/shard_map/rjkm,kjmw->rw/dot_general | solution.py:116
  239.5 28.8 %all-to-all-done.6 = f32[8,192,512]{2,1,0:T(8,128)} async-done(((f32[8,192,512]{2,1,0:T(8,128)}), f32[8,192,512]{2,1,0:T(8,128)}, u32[]{:S(2)}, u32[]{:S(2)}) %all-to-all-start.6) | async-done | bytes 3145760 | tf_op jit(solution)/shard_map/all_to_all | solution.py:115
  268.2 5.1 %all-to-all-start.3 = ((f32[8,48,512]{2,1,0:T(8,128)}), f32[8,48,512]{2,1,0:T(8,128)}, u32[]{:S(2)}, u32[]{:S(2)}) async-start(f32[8,48,512]{2,1,0:T(8,128)} %bitcast.72), calls=%async_computation.3 | async-start | bytes 1572864 | tf_op jit(solution)/shard_map/all_to_all | solution.py:43
  273.3 6.8 %fusion = f32[512,384,1,1]{0,1,3,2:T(8,128)} fusion(f32[384,4,8,48]{0,3,2,1:T(8,128)S(1)} %bitcast.64, f32[8,4,48,512]{3,2,1,0:T(8,128)} %bitcast.12), kind=kOutput, calls=%fused_computation.1 | convolution fusion | flops 3623878656 | bytes 6291456 | tf_op jit(solution)/shard_map/rjkm,kjmw->rw/dot_general | solution.py:116
  280.0 5.5 %all-to-all-done.3 = f32[8,48,512]{2,1,0:T(8,128)} async-done(((f32[8,48,512]{2,1,0:T(8,128)}), f32[8,48,512]{2,1,0:T(8,128)}, u32[]{:S(2)}, u32[]{:S(2)}) %all-to-all-start.3) | async-done | bytes 786464 | tf_op jit(solution)/shard_map/all_to_all | solution.py:43
  285.6 5.1 %all-to-all-start.7 = ((f32[8,48,512]{2,1,0:T(8,128)}), f32[8,48,512]{2,1,0:T(8,128)}, u32[]{:S(2)}, u32[]{:S(2)}) async-start(f32[8,48,512]{2,1,0:T(8,128)} %bitcast.71), calls=%async_computation.7 | async-start | bytes 1572864 | tf_op jit(solution)/shard_map/all_to_all | solution.py:43
  290.6 1.2 reduce_sum.36
  291.8 0.1 broadcast_multiply_fusion.2
  291.9 1.0 convolution_bitcast_fusion.2
  292.9 0.0 copy-done.8
  293.0 1.0 convolution_bitcast_fusion.3
  294.0 8.9 %all-to-all-done.7 = f32[8,48,512]{2,1,0:T(8,128)} async-done(((f32[8,48,512]{2,1,0:T(8,128)}), f32[8,48,512]{2,1,0:T(8,128)}, u32[]{:S(2)}, u32[]{:S(2)}) %all-to-all-start.7) | async-done | bytes 786464 | tf_op jit(solution)/shard_map/all_to_all | solution.py:43
  302.9 1.8 reduce_sum.37
  304.8 1.6 fusion.7
  306.4 0.0 copy-start.9
  306.4 1.0 convolution_bitcast_fusion.1
  307.4 0.3 copy.49
  307.7 0.3 copy.48
  308.0 0.3 copy.47
  308.3 0.0 copy-done.9
  308.3 1.8 pad_maximum_fusion
  310.1 4.5 reshape_reshape.4
  314.7 3.7 copy.40
  318.4 41.6 %all_to_all.70 = f32[8,32,3072]{2,1,0:T(8,128)} all-to-all(f32[8,32,3072]{2,1,0:T(8,128)S(1)} %copy.40), channel_id=1, replica_groups=mesh['prow_0'=4,'prow_1'=8,'pcol_0'=4,'pcol_1'=2] {'pcol_0','pcol_1'}, dimensions={0} | all-to-all | bytes 6291456 | tf_op jit(solution)/shard_map/all_to_all | solution.py:43
  360.0 2.1 reduce_sum.38
  362.0 0.3 all_to_all.51
  362.3 14.6 %all_to_all.71 = f32[32,1,3072]{2,1,0:T(1,128)S(1)} all-to-all(f32[32,1,3072]{2,1,0:T(1,128)S(1)} %all_to_all.51), channel_id=1, replica_groups=mesh['prow_0'=4,'prow_1'=8,'pcol_0'=4,'pcol_1'=2] {'prow_0','prow_1'}, dimensions={0} | all-to-all | bytes 786432 | tf_op jit(solution)/shard_map/all_to_all | solution.py:51
  376.9 0.2 reduce_sum.39
  377.1 0.2 broadcast_in_dim.24
  377.3 18.1 %all_to_all.72 = f32[32,1,3072]{2,1,0:T(1,128)S(1)} all-to-all(f32[32,1,3072]{2,1,0:T(1,128)S(1)} %broadcast_in_dim.24), channel_id=1, replica_groups=mesh['prow_0'=4,'prow_1'=8,'pcol_0'=4,'pcol_1'=2] {'prow_0','prow_1'}, dimensions={0} | all-to-all | bytes 786432 | tf_op jit(solution)/shard_map/all_to_all | solution.py:64
  395.4 0.1 copy.55
  395.5 2.0 broadcast_in_dim.25
  397.6 9.1 %all-to-all-start.11 = ((f32[8,32,3072]{2,1,0:T(8,128)}), f32[8,32,3072]{2,1,0:T(8,128)}, u32[]{:S(2)}, u32[]{:S(2)}) async-start(f32[8,32,3072]{2,1,0:T(8,128)} %broadcast_in_dim.25), calls=%async_computation.11 | async-start | bytes 6291456 | tf_op jit(solution)/shard_map/all_to_all | solution.py:64
  406.6 1.9 fusion.10
  408.5 35.7 %all-to-all-done.11 = f32[8,32,3072]{2,1,0:T(8,128)} async-done(((f32[8,32,3072]{2,1,0:T(8,128)}), f32[8,32,3072]{2,1,0:T(8,128)}, u32[]{:S(2)}, u32[]{:S(2)}) %all-to-all-start.11) | async-done | bytes 3145760 | tf_op jit(solution)/shard_map/all_to_all | solution.py:64
  444.2 5.4 %copy.41 = f32[32,8,3072]{2,1,0:T(8,128)} copy(f32[32,8,3072]{2,0,1:T(8,128)} %bitcast.18) | data formatting | bytes 6291456 | tf_op jit(solution)/shard_map/transpose | solution.py:70
  449.6 4.7 %slice.14 = f32[1536,512]{1,0:T(8,128)} reshape(f32[32,8,3072]{2,1,0:T(8,128)} %copy.41) | data formatting | bytes 6291456 | tf_op jit(solution)/shard_map/slice | solution.py:85
  454.3 3.3 convolution_subtract_fusion
  457.6 0.0 copy-start.5
  457.6 1.9 fusion.6
  459.5 0.0 copy-start.4
  459.5 2.9 fusion.5
  462.3 0.0 copy-done.4
  (16 shorter events, 0.1 us)
Async XLA Ops:
  0.6 304.1 %copy-start = (f32[512,512]{1,0:T(8,128)S(1)}, f32[512,512]{1,0:T(8,128)}, u32[]{:S(2)}) copy-start(f32[512,512]{1,0:T(8,128)} %param.11) | copy-start | bytes 3145732
  2.6 0.6 copy-start.7
  4.0 11.1 %all-to-all-start = ((f32[4,1,48,512]{3,2,1,0:T(8,128)}), f32[4,1,48,512]{3,2,1,0:T(8,128)S(1)}, u32[]{:S(2)}, u32[]{:S(2)}) async-start(f32[4,1,48,512]{3,2,1,0:T(8,128)} %stack.12), calls=%async_computation | async-start | bytes 786432 | tf_op jit(solution)/shard_map/all_to_all | solution.py:23
  104.3 73.3 %all-to-all-start.5 = ((f32[8,4,48,512]{3,2,1,0:T(8,128)}), f32[8,4,48,512]{3,2,1,0:T(8,128)}, u32[]{:S(2)}, u32[]{:S(2)}) async-start(f32[8,4,48,512]{3,2,1,0:T(8,128)} %stack.15), calls=%async_computation.5 | async-start | bytes 6291456 | tf_op jit(solution)/shard_map/all_to_all | solution.py:23
  177.5 47.8 %all-to-all-start.2 = ((f32[8,192,512]{2,1,0:T(8,128)}), f32[8,192,512]{2,1,0:T(8,128)}, u32[]{:S(2)}, u32[]{:S(2)}) async-start(f32[8,192,512]{2,1,0:T(8,128)} %bitcast.66), calls=%async_computation.2 | async-start | bytes 6291456 | tf_op jit(solution)/shard_map/all_to_all | solution.py:115
  225.4 42.9 %all-to-all-start.6 = ((f32[8,192,512]{2,1,0:T(8,128)}), f32[8,192,512]{2,1,0:T(8,128)}, u32[]{:S(2)}, u32[]{:S(2)}) async-start(f32[8,192,512]{2,1,0:T(8,128)} %bitcast.65), calls=%async_computation.6 | async-start | bytes 6291456 | tf_op jit(solution)/shard_map/all_to_all | solution.py:115
  268.2 17.4 %all-to-all-start.3 = ((f32[8,48,512]{2,1,0:T(8,128)}), f32[8,48,512]{2,1,0:T(8,128)}, u32[]{:S(2)}, u32[]{:S(2)}) async-start(f32[8,48,512]{2,1,0:T(8,128)} %bitcast.72), calls=%async_computation.3 | async-start | bytes 1572864 | tf_op jit(solution)/shard_map/all_to_all | solution.py:43
  280.0 12.9 %copy-start.8 = (f32[48,512]{1,0:T(8,128)S(1)}, f32[48,512]{1,0:T(8,128)}, u32[]{:S(2)}) copy-start(f32[48,512]{1,0:T(8,128)} %copy-done.7) | copy-start | bytes 294916
  285.6 17.3 %all-to-all-start.7 = ((f32[8,48,512]{2,1,0:T(8,128)}), f32[8,48,512]{2,1,0:T(8,128)}, u32[]{:S(2)}, u32[]{:S(2)}) async-start(f32[8,48,512]{2,1,0:T(8,128)} %bitcast.71), calls=%async_computation.7 | async-start | bytes 1572864 | tf_op jit(solution)/shard_map/all_to_all | solution.py:43
  291.9 15.8 %copy-start.6 = (f32[48,512]{1,0:T(8,128)}, f32[48,512]{1,0:T(8,128)S(1)}, u32[]{:S(2)}) copy-start(f32[48,512]{1,0:T(8,128)S(1)} %broadcast_multiply_fusion.2) | copy-start | bytes 294916
  306.4 1.9 copy-start.9
  397.6 9.1 %copy-start.2 = (f32[512,512]{1,0:T(8,128)S(1)}, f32[512,512]{1,0:T(8,128)}, u32[]{:S(2)}) copy-start(f32[512,512]{1,0:T(8,128)} %param.13) | copy-start | bytes 3145732
  397.6 46.6 %all-to-all-start.11 = ((f32[8,32,3072]{2,1,0:T(8,128)}), f32[8,32,3072]{2,1,0:T(8,128)}, u32[]{:S(2)}, u32[]{:S(2)}) async-start(f32[8,32,3072]{2,1,0:T(8,128)} %broadcast_in_dim.25), calls=%async_computation.11 | async-start | bytes 6291456 | tf_op jit(solution)/shard_map/all_to_all | solution.py:64
  449.6 4.7 %copy-start.3 = (f32[512,512]{1,0:T(8,128)S(1)}, f32[512,512]{1,0:T(8,128)}, u32[]{:S(2)}) copy-start(f32[512,512]{1,0:T(8,128)} %param.12) | copy-start | bytes 3145732
  454.3 3.3 copy-start.1
  457.6 4.8 %copy-start.5 = (f32[512,512]{1,0:T(8,128)}, f32[512,512]{1,0:T(8,128)S(1)}, u32[]{:S(2)}) copy-start(f32[512,512]{1,0:T(8,128)S(1)} %convolution_subtract_fusion) | copy-start | bytes 3145732
  459.5 2.9 copy-start.4
